TPU v7x, 32 devices: a whole 2x2x4 slice. The times are simulated.
32 devices in a mesh: blk: 8 (over y, x, core), frq: 4 (over z).
Axes of the slice: x: 2, y: 2, z: 4, core: 2. Of those that a mesh axis runs over, the one named last changes fastest.
Arguments:
- spectra: bfloat16 [2, 1024, 64, 512], P(None, 'blk', None, 'frq'), may hold values from -6 to 6
- live: int32 [1024], P('blk'), may hold values 0 or 1
Outputs:
- xcorr: float32 [3, 1024, 128, 128], P(None, ('blk', 'frq'))
All inputs are finite; a program needn't handle non-finite values. No bound on the sum of `live` on one device may be relied on, other than what follows from the above.
Results may differ from a plain program's by a relative error of at most 0.0058.
Values may be sent and summed in bfloat16 or wider, within the bound.
No kernel may reach another device: no remote copies, remote signals or barrier semaphores. Data moves between devices by JAX's collectives and lax.ppermute only.
A program may use at most 128 MiB of HBM per device.

v0:
```python
import math

import jax
import jax.numpy as jnp
from jax import lax
from jax.sharding import PartitionSpec as P

F = 512
W = 64
LAGS = 128
ROUNDS = 3


EPSILON = 1e-06


def shifted(shard, axis, by):
    length = lax.axis_size(axis)
    return lax.ppermute(shard, axis, [(i, (i + by) % length) for i in range(length)])


def normalize(spectra, live):
    values = spectra.astype(jnp.float32)
    energy = jnp.mean(values * values, axis=(0, 2), keepdims=True)
    weight = live.astype(jnp.float32)[None, :, None, None] * lax.rsqrt(energy + EPSILON)
    return (values * weight).astype(jnp.bfloat16)


def lag_table(first_bin, bin_count, length_all, lag_count):
    bins = first_bin + jnp.arange(bin_count, dtype=jnp.int32)
    delays = jnp.arange(lag_count, dtype=jnp.int32) - lag_count // 2
    residue = jnp.mod(bins[:, None] * delays[None, :], 2 * length_all)
    phases = residue.astype(jnp.float32) * (math.pi / length_all)
    factor = 1.0 / math.sqrt(length_all)
    return jnp.stack([jnp.cos(phases) * factor, -jnp.sin(phases) * factor], 0).astype(jnp.bfloat16)


def cross_block(local_block, remote_block):

    def product(left, right):
        return jnp.einsum("cwf,dwf->cdf", left, right, preferred_element_type=jnp.float32)

    factor = 1.0 / math.sqrt(W)
    real_part = (
        product(local_block[0], remote_block[0]) + product(local_block[1], remote_block[1])
    ) * factor
    imag_part = (
        product(local_block[1], remote_block[0]) - product(local_block[0], remote_block[1])
    ) * factor
    return jnp.stack([real_part, imag_part], axis=2).astype(jnp.bfloat16)


def local(spectra, live):
    normed = normalize(spectra, live)
    local_bins = spectra.shape[3]
    rows_here = spectra.shape[1] // lax.axis_size("frq")
    used_table = lag_table(lax.axis_index("frq") * local_bins, local_bins, F, LAGS)
    outputs = []
    partner = normed
    for offset in range(1, ROUNDS + 1):
        partner = shifted(partner, "blk", -1)
        cross_spec = cross_block(normed, partner)

        def partial_time(first_row, row_count, source=cross_spec):
            return jnp.einsum(
                "cdpf,pfl->cdl", source, used_table, preferred_element_type=jnp.float32
            )

        lagged = lax.psum_scatter(
            partial_time(jnp.int32(0), rows_here * lax.axis_size("frq")),
            "frq",
            scatter_dimension=0,
            tiled=True,
        )
        outputs.append(lagged)
    return jnp.stack(outputs, 0)


def solution(mesh):
    return jax.shard_map(
        local,
        mesh=mesh,
        in_specs=(P(None, "blk", None, "frq"), P("blk")),
        out_specs=P(None, ("blk", "frq"), None, None),
        check_vma=False,
    )
```

profile of v0, /device:TPU:0, one launch (start us, length us, event | category | flops | bytes accessed | tf_op | source)
XLA Modules:
  0.0 570.8 jit_solution(5201168471966087683)
XLA Ops:
  6.5 7.3 %copy.3 = bf16[2,128,64,128]{1,2,3,0:T(8,128)(2,1)} copy(bf16[2,128,64,128]{3,2,1,0:T(8,128)(2,1)} %param.2) | data formatting | bytes 8388608 | tf_op args[0]
  24.4 46.0 %collective-permute-done = bf16[2,128,64,128]{1,2,3,0:T(8,128)(2,1)} collective-permute-done((bf16[2,128,64,128]{1,2,3,0:T(8,128)(2,1)}, bf16[2,128,64,128]{1,2,3,0:T(8,128)(2,1)}, u32[]{:S(2)}, u32[]{:S(2)}) %collective-permute-start) | collective-permute-done | bytes 4194336 | tf_op jit(solution)/shard_map/ppermute | solution.py:19
  77.4 4.1 fusion.2
  81.5 6.0 %fusion.3 = bf16[128,128,1,128]{0,1,3,2:T(8,128)(2,1)} fusion(f32[128,128,128]{2,1,0:T(8,128)S(1)} %fusion.8, bf16[2,128,64,128]{1,2,3,0:T(8,128)(2,1)} %collective-permute-done, bf16[2,128,64,128]{1,2,3,0:T(8,128)(2,1)} %fusion.1), kind=kOutput, calls=%fused_computation.15 | convolution fusion | flops 274726912 | bytes 16777216 | tf_op jit(solution)/shard_map/cwf,dwf->cdf/dot_general | solution.py:41
  87.5 6.2 %pad_maximum_fusion = bf16[128,128,2,128]{0,1,3,2:T(8,128)(2,1)} fusion(bf16[128,128,1,128]{0,1,3,2:T(8,128)(2,1)} %fusion.3, bf16[128,128,1,128]{0,1,3,2:T(8,128)(2,1)S(1)} %fusion.2), kind=kLoop, calls=%fused_computation.4 | loop fusion | flops 4194304 | bytes 16777216 | tf_op jit(solution)/shard_map/stack | solution.py:50
  93.7 13.5 %copy.4 = bf16[128,128,2,128]{3,1,2,0:T(8,128)(2,1)} copy(bf16[128,128,2,128]{0,1,3,2:T(8,128)(2,1)} %pad_maximum_fusion) | data formatting | bytes 16777216 | tf_op jit(solution)/shard_map/stack | solution.py:50
  107.3 8.9 %convolution_bitcast_fusion.2 = f32[128,128,128]{2,1,0:T(8,128)} fusion(bf16[128,128,2,128]{3,1,2,0:T(8,128)(2,1)} %copy.4, bf16[1,128,128]{2,1,0:T(8,128)(2,1)S(1)} %get-tuple-element.6, bf16[1,128,128]{2,1,0:T(8,128)(2,1)S(1)} %get-tuple-element.5), kind=kOutput, calls=%fused_computation.22 | convolution fusion | flops 1073774592 | bytes 16842752 | tf_op jit(solution)/shard_map/cdpf,pfl->cdl/dot_general | solution.py:65
  119.4 46.3 %collective-permute-done.1 = bf16[2,128,64,128]{1,2,3,0:T(8,128)(2,1)S(1)} collective-permute-done((bf16[2,128,64,128]{1,2,3,0:T(8,128)(2,1)}, bf16[2,128,64,128]{1,2,3,0:T(8,128)(2,1)S(1)}, u32[]{:S(2)}, u32[]{:S(2)}) %collective-permute-start.1) | collective-permute-done | bytes 4194336 | tf_op jit(solution)/shard_map/ppermute | solution.py:19
  165.7 4.4 fusion.11
  173.1 4.1 fusion.4
  177.2 6.3 %fusion.5 = bf16[128,128,1,128]{0,1,3,2:T(8,128)(2,1)} fusion(f32[128,128,128]{2,1,0:T(8,128)S(1)} %fusion.10, bf16[2,128,64,128]{1,2,3,0:T(8,128)(2,1)} %copy-done.1, bf16[2,128,64,128]{1,2,3,0:T(8,128)(2,1)} %fusion.1), kind=kOutput, calls=%fused_computation.17 | convolution fusion | flops 274726912 | bytes 16777216 | tf_op jit(solution)/shard_map/cwf,dwf->cdf/dot_general | solution.py:41
  183.4 6.3 %pad_maximum_fusion.1 = bf16[128,128,2,128]{0,1,3,2:T(8,128)(2,1)} fusion(bf16[128,128,1,128]{0,1,3,2:T(8,128)(2,1)} %fusion.5, bf16[128,128,1,128]{0,1,3,2:T(8,128)(2,1)S(1)} %fusion.4), kind=kLoop, calls=%fused_computation.5 | loop fusion | flops 4194304 | bytes 16777216 | tf_op jit(solution)/shard_map/stack | solution.py:50
  189.8 13.6 %copy.5 = bf16[128,128,2,128]{3,1,2,0:T(8,128)(2,1)} copy(bf16[128,128,2,128]{0,1,3,2:T(8,128)(2,1)} %pad_maximum_fusion.1) | data formatting | bytes 16777216 | tf_op jit(solution)/shard_map/stack | solution.py:50
  203.3 9.0 %convolution_bitcast_fusion.1 = f32[128,128,128]{2,1,0:T(8,128)} fusion(bf16[128,128,2,128]{3,1,2,0:T(8,128)(2,1)} %copy.5, bf16[1,128,128]{2,1,0:T(8,128)(2,1)S(1)} %get-tuple-element.6, bf16[1,128,128]{2,1,0:T(8,128)(2,1)S(1)} %get-tuple-element.5), kind=kOutput, calls=%fused_computation.21 | convolution fusion | flops 1073774592 | bytes 16842752 | tf_op jit(solution)/shard_map/cdpf,pfl->cdl/dot_general | solution.py:65
  215.1 46.3 %collective-permute-done.2 = bf16[2,128,64,128]{1,2,3,0:T(8,128)(2,1)S(1)} collective-permute-done((bf16[2,128,64,128]{1,2,3,0:T(8,128)(2,1)}, bf16[2,128,64,128]{1,2,3,0:T(8,128)(2,1)S(1)}, u32[]{:S(2)}, u32[]{:S(2)}) %collective-permute-start.2) | collective-permute-done | bytes 4194336 | tf_op jit(solution)/shard_map/ppermute | solution.py:19
  261.4 4.5 fusion.13
  268.8 4.1 fusion.6
  272.9 6.0 %fusion.7 = bf16[128,128,1,128]{0,1,3,2:T(8,128)(2,1)} fusion(f32[128,128,128]{2,1,0:T(8,128)S(1)} %fusion.12, bf16[2,128,64,128]{1,2,3,0:T(8,128)(2,1)} %copy-done.2, bf16[2,128,64,128]{1,2,3,0:T(8,128)(2,1)} %fusion.1), kind=kOutput, calls=%fused_computation.19 | convolution fusion | flops 274726912 | bytes 16777216 | tf_op jit(solution)/shard_map/cwf,dwf->cdf/dot_general | solution.py:41
  278.9 6.2 %pad_maximum_fusion.2 = bf16[128,128,2,128]{0,1,3,2:T(8,128)(2,1)} fusion(bf16[128,128,1,128]{0,1,3,2:T(8,128)(2,1)} %fusion.7, bf16[128,128,1,128]{0,1,3,2:T(8,128)(2,1)S(1)} %fusion.6), kind=kLoop, calls=%fused_computation.6 | loop fusion | flops 4194304 | bytes 16777216 | tf_op jit(solution)/shard_map/stack | solution.py:50
  285.1 13.5 %copy.6 = bf16[128,128,2,128]{3,1,2,0:T(8,128)(2,1)} copy(bf16[128,128,2,128]{0,1,3,2:T(8,128)(2,1)} %pad_maximum_fusion.2) | data formatting | bytes 16777216 | tf_op jit(solution)/shard_map/stack | solution.py:50
  298.7 9.0 %convolution_bitcast_fusion = f32[128,128,128]{2,1,0:T(8,128)} fusion(bf16[128,128,2,128]{3,1,2,0:T(8,128)(2,1)} %copy.6, bf16[1,128,128]{2,1,0:T(8,128)(2,1)S(1)} %get-tuple-element.6, bf16[1,128,128]{2,1,0:T(8,128)(2,1)S(1)} %get-tuple-element.5), kind=kOutput, calls=%fused_computation.20 | convolution fusion | flops 1073774592 | bytes 16842752 | tf_op jit(solution)/shard_map/cdpf,pfl->cdl/dot_general | solution.py:65
  307.7 102.5 %reduce-scatter.6.cloned.1.call-done = f32[32,128,128]{2,1,0:T(8,128)} async-done(((f32[128,128,128]{2,1,0:T(8,128)}), f32[32,128,128]{2,1,0:T(8,128)}) %reduce-scatter.6.cloned.1.call-update) | async-done | bytes 2097168 | tf_op jit(solution)/shard_map/reduce_scatter | solution.py:69
  410.3 147.6 %reduce-scatter.8.cloned.1.call-done = f32[32,128,128]{2,1,0:T(8,128)} async-done(((f32[128,128,128]{2,1,0:T(8,128)}), f32[32,128,128]{2,1,0:T(8,128)}) %reduce-scatter.8.cloned.1.call-update) | async-done | bytes 2097168 | tf_op jit(solution)/shard_map/reduce_scatter | solution.py:69
  557.9 6.4 %pad_maximum_fusion.3 = f32[3,32,128,128]{3,2,1,0:T(8,128)} fusion(f32[1,32,128,128]{3,2,1,0:T(8,128)} %bitcast.86, f32[1,32,128,128]{3,2,1,0:T(8,128)} %bitcast.85, f32[1,32,128,128]{3,2,1,0:T(8,128)} %bitcast.84), kind=kLoop, calls=%fused_computation.13 | loop fusion | flops 3145728 | bytes 12582912 | tf_op jit(solution)/shard_map/stack | solution.py:76
  (28 shorter events, 29.4 us)
Async XLA Ops:
  6.5 301.2 %reduce-scatter.4.cloned.1.call-start = ((), (), s32[]{:S(2)}) async-start(), calls=%async_computation.3 | async-start | bytes 10485760 | tf_op jit(solution)/shard_map/reduce_scatter | solution.py:69
  13.8 3.6 copy-start.3
  13.8 3.6 copy-start
  20.6 49.7 %collective-permute-start = (bf16[2,128,64,128]{1,2,3,0:T(8,128)(2,1)}, bf16[2,128,64,128]{1,2,3,0:T(8,128)(2,1)}, u32[]{:S(2)}, u32[]{:S(2)}) collective-permute-start(bf16[2,128,64,128]{1,2,3,0:T(8,128)(2,1)} %fusion.1), channel_id=1, source_target_pairs={{0,28},{4,0},{8,4},{12,8},{16,12},{20,16},{24,20},{28,24},{1,29},{... | collective-permute-start | bytes 12582920 | tf_op jit(solution)/shard_map/ppermute | solution.py:19
  116.2 294.0 %reduce-scatter.6.cloned.1.call-start = ((), (), s32[]{:S(2)}) async-start(), calls=%async_computation.4 | async-start | bytes 10485760 | tf_op jit(solution)/shard_map/reduce_scatter | solution.py:69
  116.3 49.4 %collective-permute-start.1 = (bf16[2,128,64,128]{1,2,3,0:T(8,128)(2,1)}, bf16[2,128,64,128]{1,2,3,0:T(8,128)(2,1)S(1)}, u32[]{:S(2)}, u32[]{:S(2)}) collective-permute-start(bf16[2,128,64,128]{1,2,3,0:T(8,128)(2,1)} %collective-permute-done), channel_id=1, source_target_pairs={{0,28},{4,0},{8,4},{12,8},{16,12},{20,16},{24,20},{28,24},{1,29},{... | collective-permute-start | bytes 12582920 | tf_op jit(solution)/shard_map/ppermute | solution.py:19
  165.7 4.5 copy-start.1
  212.3 345.6 %reduce-scatter.8.cloned.1.call-start = ((), (), s32[]{:S(2)}) async-start(), calls=%async_computation.5 | async-start | bytes 10485760 | tf_op jit(solution)/shard_map/reduce_scatter | solution.py:69
  212.4 49.1 %collective-permute-start.2 = (bf16[2,128,64,128]{1,2,3,0:T(8,128)(2,1)}, bf16[2,128,64,128]{1,2,3,0:T(8,128)(2,1)S(1)}, u32[]{:S(2)}, u32[]{:S(2)}) collective-permute-start(bf16[2,128,64,128]{1,2,3,0:T(8,128)(2,1)} %copy-done.1), channel_id=1, source_target_pairs={{0,28},{4,0},{8,4},{12,8},{16,12},{20,16},{24,20},{28,24},{1,29},{... | collective-permute-start | bytes 12582920 | tf_op jit(solution)/shard_map/ppermute | solution.py:19
  261.4 4.5 copy-start.2
Sparse Core Ops, SparseCore 0:
  116.3 146.2 reduce-scatter.3
  265.0 145.2 reduce-scatter.5
  412.6 145.2 reduce-scatter.7
where the time goes:
time: 572 us; the launch traced here: 571 us
  waiting for transfers between devices  389 us (68%)
  matrix products  79.3 us (14%)
  local copies, waits for them, and re-layouts  48 us (8%)
  other arithmetic  32.1 us (6%)
  between operations  13.2 us (2%)
  starting transfers between devices  9.26 us (2%)
    reduce_scatter x3, waiting for transfers between devices, local(): lax.psum_scatter(partial_time(jnp.int32(0), rows_here * lax.axis_size('fr...  250 us
    ppermute x3, waiting for transfers between devices, shifted(): lax.ppermute(shard, axis, [(i, (i + by) % length) for i in range(length)])  139 us
    dot_general x12, matrix products, product(): jnp.einsum('cwf,dwf->cdf', left, right, preferred_element_type=jnp.float32)  52.4 us
    another operation x3, local copies, waits for them, and re-layouts, cross_block(): return jnp.stack([real_part, imag_part], axis=2).astype(jnp.bfloat16)  40.7 us
    dot_general x3, matrix products, partial_time(): jnp.einsum('cdpf,pfl->cdl', source, used_table, preferred_element_type=jn...  26.9 us
    another operation x3, other arithmetic, cross_block(): return jnp.stack([real_part, imag_part], axis=2).astype(jnp.bfloat16)  18.7 us
  transfers between devices with their start and end apart: 6, of which 5 were waited for; matrix products, arithmetic and copies ran while one was open for 16% of the time, Pallas kernels for 0%

commit v1 on v0

v1 whole, which is shorter than its diff:
```python
import functools, math
import jax, jax.numpy as jnp
from jax import lax
from jax.experimental import pallas as pl
from jax.experimental.pallas import tpu as pltpu
from jax.sharding import PartitionSpec as P

EPSILON = 1e-06
GROUP = 16

def prep_kernel(first, live_ref, x_ref, out_ref, turned):
    parts, group, windows, bins = x_ref.shape
    taps = parts * windows
    start = (first + pl.program_id(0)) * group
    for c in range(group):
        x = x_ref[:, c].astype(jnp.float32).reshape(taps, bins)
        energy = jnp.sum(x * x, axis=0, keepdims=True) * (1.0 / taps)
        weight = live_ref[start + c].astype(jnp.float32) * lax.rsqrt(energy + EPSILON)
        turned[pl.ds(c, bins, stride=group), :] = (x * weight).T
    out_ref[...] = turned[...].reshape(bins, group, taps).astype(jnp.bfloat16)

def prepared(spectra, live, first, count):
    parts, channels, windows, bins = spectra.shape
    taps = parts * windows
    return pl.pallas_call(
        functools.partial(prep_kernel, first // GROUP),
        grid_spec=pltpu.PrefetchScalarGridSpec(
            num_scalar_prefetch=1,
            grid=(count // GROUP,),
            in_specs=[pl.BlockSpec((parts, GROUP, windows, bins), lambda g, live: (0, first // GROUP + g, 0, 0))],
            out_specs=pl.BlockSpec((bins, GROUP, taps), lambda g, live: (0, g, 0)),
            scratch_shapes=[pltpu.VMEM((bins * GROUP, taps), jnp.float32)],
        ),
        out_shape=jax.ShapeDtypeStruct((bins, count, taps), jnp.bfloat16),
        compiler_params=pltpu.CompilerParams(vmem_limit_bytes=32 << 20),
        cost_estimate=pl.CostEstimate(flops=4 * bins * count * taps * 256, bytes_accessed=4 * bins * count * taps, transcendentals=0),
        name="prep",
    )(live, spectra)

FB = 16
IB = 16

def cross_kernel(steps, pitch, *refs):
    *locals_, b_ref, table_ref, out_ref, held = refs
    fb, js, taps = b_ref.shape
    half = taps // 2
    step = pl.program_id(0)
    rows = sum(a.shape[1] for a in locals_)
    bins = steps * fb

    @pl.when(step < steps)
    def _():
        for k in range(fb):
            b = b_ref[k]
            twisted = jnp.concatenate([-b[:, half:], b[:, :half]], axis=1)
            both = jnp.concatenate([b, twisted], axis=0)
            at = 0
            for a in locals_:
                n = a.shape[1]
                c = lax.dot_general(a[k], both, (((1,), (1,)), ((), ())), preferred_element_type=jnp.float32)
                held[pl.ds(at * pitch + step * fb + k, n, stride=pitch), :] = c
                at += n

    @pl.when(step >= steps)
    def _():
        ib = out_ref.shape[0]
        first = (step - steps) * ib
        scale = 1.0 / math.sqrt(half)
        pieces = []
        for i in range(ib):
            x = held[pl.ds((first + i) * pitch, bins), :]
            xt = (x * scale).astype(jnp.bfloat16).T
            pieces.append(jnp.concatenate([xt[:js], xt[js:]], axis=1))
        lhs = jnp.concatenate(pieces, axis=0)
        y = jnp.dot(lhs, table_ref[...], preferred_element_type=jnp.float32)
        out_ref[...] = y.reshape(out_ref.shape).astype(out_ref.dtype)

def crossed(local_chunks, partner, table, fb=FB, ib=IB, pad=4):
    bins, js, taps = partner.shape
    rows = sum(a.shape[1] for a in local_chunks)
    lags = table.shape[1]
    steps = bins // fb
    pitch = bins + pad
    last = steps - 1
    return pl.pallas_call(
        functools.partial(cross_kernel, steps, pitch),
        grid=(steps + rows // ib,),
        in_specs=[pl.BlockSpec((fb, a.shape[1], taps), lambda s: (jnp.minimum(s, last), 0, 0)) for a in local_chunks]
        + [
            pl.BlockSpec((fb, js, taps), lambda s: (jnp.minimum(s, last), 0, 0)),
            pl.BlockSpec(table.shape, lambda s: (0, 0)),
        ],
        out_specs=pl.BlockSpec((ib, js, lags), lambda s: (jnp.maximum(s - steps, 0), 0, 0)),
        out_shape=jax.ShapeDtypeStruct((rows, js, lags), jnp.bfloat16),
        scratch_shapes=[pltpu.VMEM((rows * pitch, 2 * js), jnp.float32)],
        compiler_params=pltpu.CompilerParams(vmem_limit_bytes=48 << 20),
        cost_estimate=pl.CostEstimate(flops=8 * rows * js * bins * taps, bytes_accessed=2 * bins * taps * (rows + js) + 2 * rows * js * lags, transcendentals=0),
        name="cross",
    )(*local_chunks, partner, table)


F = 512
ROUNDS = 3
LAGS = 128
CHUNKS = 2


def shifted(shard, axis, by):
    length = lax.axis_size(axis)
    return lax.ppermute(shard, axis, [(i, (i + by) % length) for i in range(length)])


def lag_table(first_bin, bin_count, length_all, lag_count):
    bins = first_bin + jnp.arange(bin_count, dtype=jnp.int32)
    delays = jnp.arange(lag_count, dtype=jnp.int32) - lag_count // 2
    residue = jnp.mod(bins[:, None] * delays[None, :], 2 * length_all)
    phases = residue.astype(jnp.float32) * (math.pi / length_all)
    factor = 1.0 / math.sqrt(length_all)
    return jnp.concatenate([jnp.cos(phases) * factor, -jnp.sin(phases) * factor], 0).astype(jnp.bfloat16)


def local(spectra, live):
    channels, bins = spectra.shape[1], spectra.shape[3]
    share = channels // CHUNKS
    table = lag_table(lax.axis_index("frq") * bins, bins, F, LAGS)
    mine = [prepared(spectra, live, n * share, share) for n in range(CHUNKS)]
    partner = list(mine)
    outputs = []
    for _ in range(ROUNDS):
        pieces = []
        for n in range(CHUNKS):
            partner[n] = shifted(partner[n], "blk", -1)
            partial_sum = crossed(mine, partner[n], table)
            pieces.append(lax.psum_scatter(partial_sum, "frq", scatter_dimension=0, tiled=True))
        outputs.append(jnp.concatenate(pieces, axis=1).astype(jnp.float32))
    return jnp.stack(outputs, 0)


def solution(mesh):
    return jax.shard_map(
        local,
        mesh=mesh,
        in_specs=(P(None, "blk", None, "frq"), P("blk")),
        out_specs=P(None, ("blk", "frq"), None, None),
        check_vma=False,
    )
```

time: 572 us -> 336 us (0.59)
  waiting for transfers between devices: 389 us -> 200 us
  matrix products: 79.3 us -> 0 us
  Pallas kernels: 0 us -> 75.8 us
  other arithmetic: 32.1 us -> 4.77 us
  local copies, waits for them, and re-layouts: 48 us -> 21.2 us
  starting transfers between devices: 9.26 us -> 18.6 us
    reduce_scatter x3 -> x6, waiting for transfers between devices: 250 us -> 64.4 us  [local(): lax.psum_scatter(partial_sum, 'frq', scatter_dimension=0, tiled=True)]
    dot_general x15 -> x0, matrix products: 79.3 us -> none  [the longest x12 52.4 us: product(): jnp.einsum('cwf,dwf->cdf', left, right, preferred_element_type=jnp.float32)]
    pallas_call x0 -> x8, Pallas kernels: none -> 75.8 us  [the longest x6 69.7 us: crossed(): pl.pallas_call(functools.partial(cross_kernel, steps, pitch), grid=(steps...]
    another operation x3 -> x0, local copies, waits for them, and re-layouts: 40.7 us -> none  [cross_block(): return jnp.stack([real_part, imag_part], axis=2).astype(jnp.bfloat16)]
    another operation x4 -> x1, other arithmetic: 19 us -> 0.35 us  [the longest x3 18.7 us: cross_block(): return jnp.stack([real_part, imag_part], axis=2).astype(jnp.bfloat16)]
    unnamed x9 -> x32, local copies, waits for them, and re-layouts: 7.32 us -> 21.2 us
    ppermute x3 -> x6, starting transfers between devices: 9.17 us -> 18.4 us  [shifted(): lax.ppermute(shard, axis, [(i, (i + by) % length) for i in range(length)])]
    ppermute x3 -> x6, waiting for transfers between devices: 139 us -> 136 us  [shifted(): lax.ppermute(shard, axis, [(i, (i + by) % length) for i in range(length)])]
  transfers between devices with their start and end apart: 6 -> 12, of which waited for: 5 -> 8; matrix products, arithmetic and copies ran while one was open for 16% -> 0% of each run, Pallas kernels for 0% -> 18%
where the time goes in v1:
time: 336 us; the launch traced here: 334 us
  waiting for transfers between devices  200 us (60%)
  Pallas kernels  75.8 us (23%)
  local copies, waits for them, and re-layouts  21.2 us (6%)
  starting transfers between devices  18.6 us (6%)
  between operations  13.7 us (4%)
  other arithmetic  4.77 us (1%)
    ppermute x6, waiting for transfers between devices, shifted(): lax.ppermute(shard, axis, [(i, (i + by) % length) for i in range(length)])  136 us
    pallas_call x6, Pallas kernels, crossed(): pl.pallas_call(functools.partial(cross_kernel, steps, pitch), grid=(steps...  69.7 us
    reduce_scatter x6, waiting for transfers between devices, local(): lax.psum_scatter(partial_sum, 'frq', scatter_dimension=0, tiled=True)  64.4 us
    unnamed x32, local copies, waits for them, and re-layouts  21.2 us
    ppermute x6, starting transfers between devices, shifted(): lax.ppermute(shard, axis, [(i, (i + by) % length) for i in range(length)])  18.4 us
  transfers between devices with their start and end apart: 12, of which 8 were waited for; matrix products, arithmetic and copies ran while one was open for 0% of the time, Pallas kernels for 18%

profile of v1, /device:TPU:0, one launch (start us, length us, event | category | flops | bytes accessed | tf_op | source)
XLA Modules:
  0.0 334.5 jit_solution(2121717867311262299)
XLA Ops:
  9.4 3.0 prep.2.refs_0_
  12.4 3.4 %collective-permute-start = (bf16[128,64,128]{2,1,0:T(8,128)(2,1)S(1)}, bf16[128,64,128]{2,1,0:T(8,128)(2,1)}, u32[]{:S(2)}, u32[]{:S(2)}) collective-permute-start(bf16[128,64,128]{2,1,0:T(8,128)(2,1)S(1)} %prep.2.refs_0_), channel_id=1, source_target_pairs={{0,28},{4,0},{8,4},{12,8},{16,12},{20,16},{24,20},{28,24},{1,29},{... | collective-permute-start | bytes 6291464 | tf_op jit(solution)/shard_map/ppermute | solution.py:110
  15.9 2.2 copy-done.2
  18.0 3.1 prep.3.refs_1_
  22.8 16.6 %collective-permute-done.refs_2_ = bf16[128,64,128]{2,1,0:T(8,128)(2,1)} collective-permute-done((bf16[128,64,128]{2,1,0:T(8,128)(2,1)S(1)}, bf16[128,64,128]{2,1,0:T(8,128)(2,1)}, u32[]{:S(2)}, u32[]{:S(2)}) %collective-permute-start) | collective-permute-done | bytes 2097184 | tf_op jit(solution)/shard_map/ppermute | solution.py:110
  39.4 11.6 %cross.6 = bf16[128,64,128]{2,1,0:T(8,128)(2,1)S(1)} custom-call(bf16[128,64,128]{2,1,0:T(8,128)(2,1)S(1)} %prep.2.refs_0_, bf16[128,64,128]{2,1,0:T(8,128)(2,1)} %copy-done, bf16[128,64,128]{2,1,0:T(8,128)(2,1)} %collective-permute-done.refs_2_, bf16[256,128]{1,0:T(8,128)(2,1)S(1)} %pad_maximum_fusion.refs_3_), custom_call_target="tpu_custom_call" | custom-call | flops 1073741824 | bytes 8388608 | tf_op jit(solution)/shard_map/cross/pallas_call | solution.py:85
  52.4 3.0 collective-permute-start.1
  55.4 23.9 %collective-permute-done.1.refs_2_ = bf16[128,64,128]{2,1,0:T(8,128)(2,1)S(1)} collective-permute-done((bf16[128,64,128]{2,1,0:T(8,128)(2,1)}, bf16[128,64,128]{2,1,0:T(8,128)(2,1)S(1)}, u32[]{:S(2)}, u32[]{:S(2)}) %collective-permute-start.1) | collective-permute-done | bytes 2097184 | tf_op jit(solution)/shard_map/ppermute | solution.py:110
  80.6 11.6 %cross.7 = bf16[128,64,128]{2,1,0:T(8,128)(2,1)S(1)} custom-call(bf16[128,64,128]{2,1,0:T(8,128)(2,1)S(1)} %prep.2.refs_0_, bf16[128,64,128]{2,1,0:T(8,128)(2,1)} %copy-done, bf16[128,64,128]{2,1,0:T(8,128)(2,1)} %copy-done.13, bf16[256,128]{1,0:T(8,128)(2,1)S(1)} %pad_maximum_fusion.refs_3_), custom_call_target="tpu_custom_call" | custom-call | flops 1073741824 | bytes 8388608 | tf_op jit(solution)/shard_map/cross/pallas_call | solution.py:85
  93.7 2.9 collective-permute-start.2
  96.5 23.9 %collective-permute-done.2.refs_2_ = bf16[128,64,128]{2,1,0:T(8,128)(2,1)S(1)} collective-permute-done((bf16[128,64,128]{2,1,0:T(8,128)(2,1)}, bf16[128,64,128]{2,1,0:T(8,128)(2,1)S(1)}, u32[]{:S(2)}, u32[]{:S(2)}) %collective-permute-start.2) | collective-permute-done | bytes 2097184 | tf_op jit(solution)/shard_map/ppermute | solution.py:110
  121.8 11.6 %cross.8 = bf16[128,64,128]{2,1,0:T(8,128)(2,1)S(1)} custom-call(bf16[128,64,128]{2,1,0:T(8,128)(2,1)S(1)} %prep.2.refs_0_, bf16[128,64,128]{2,1,0:T(8,128)(2,1)} %copy-done, bf16[128,64,128]{2,1,0:T(8,128)(2,1)} %copy-done.12, bf16[256,128]{1,0:T(8,128)(2,1)S(1)} %pad_maximum_fusion.refs_3_), custom_call_target="tpu_custom_call" | custom-call | flops 1073741824 | bytes 8388608 | tf_op jit(solution)/shard_map/cross/pallas_call | solution.py:85
  134.8 3.2 collective-permute-start.3
  138.0 23.9 %collective-permute-done.3.refs_2_ = bf16[128,64,128]{2,1,0:T(8,128)(2,1)S(1)} collective-permute-done((bf16[128,64,128]{2,1,0:T(8,128)(2,1)}, bf16[128,64,128]{2,1,0:T(8,128)(2,1)S(1)}, u32[]{:S(2)}, u32[]{:S(2)}) %collective-permute-start.3) | collective-permute-done | bytes 2097184 | tf_op jit(solution)/shard_map/ppermute | solution.py:110
  163.2 11.6 %cross.9 = bf16[128,64,128]{2,1,0:T(8,128)(2,1)S(1)} custom-call(bf16[128,64,128]{2,1,0:T(8,128)(2,1)S(1)} %prep.2.refs_0_, bf16[128,64,128]{2,1,0:T(8,128)(2,1)} %copy-done, bf16[128,64,128]{2,1,0:T(8,128)(2,1)} %copy-done.11, bf16[256,128]{1,0:T(8,128)(2,1)S(1)} %pad_maximum_fusion.refs_3_), custom_call_target="tpu_custom_call" | custom-call | flops 1073741824 | bytes 8388608 | tf_op jit(solution)/shard_map/cross/pallas_call | solution.py:85
  176.3 2.8 collective-permute-start.4
  179.1 23.9 %collective-permute-done.4.refs_2_ = bf16[128,64,128]{2,1,0:T(8,128)(2,1)S(1)} collective-permute-done((bf16[128,64,128]{2,1,0:T(8,128)(2,1)}, bf16[128,64,128]{2,1,0:T(8,128)(2,1)S(1)}, u32[]{:S(2)}, u32[]{:S(2)}) %collective-permute-start.4) | collective-permute-done | bytes 2097184 | tf_op jit(solution)/shard_map/ppermute | solution.py:110
  204.4 11.6 %cross.10 = bf16[128,64,128]{2,1,0:T(8,128)(2,1)S(1)} custom-call(bf16[128,64,128]{2,1,0:T(8,128)(2,1)S(1)} %prep.2.refs_0_, bf16[128,64,128]{2,1,0:T(8,128)(2,1)} %copy-done, bf16[128,64,128]{2,1,0:T(8,128)(2,1)} %copy-done.15, bf16[256,128]{1,0:T(8,128)(2,1)S(1)} %pad_maximum_fusion.refs_3_), custom_call_target="tpu_custom_call" | custom-call | flops 1073741824 | bytes 8388608 | tf_op jit(solution)/shard_map/cross/pallas_call | solution.py:85
  217.5 3.2 collective-permute-start.5
  220.6 23.9 %collective-permute-done.5.refs_2_ = bf16[128,64,128]{2,1,0:T(8,128)(2,1)S(1)} collective-permute-done((bf16[128,64,128]{2,1,0:T(8,128)(2,1)}, bf16[128,64,128]{2,1,0:T(8,128)(2,1)S(1)}, u32[]{:S(2)}, u32[]{:S(2)}) %collective-permute-start.5) | collective-permute-done | bytes 2097184 | tf_op jit(solution)/shard_map/ppermute | solution.py:110
  245.8 11.6 %cross.11 = bf16[128,64,128]{2,1,0:T(8,128)(2,1)S(1)} custom-call(bf16[128,64,128]{2,1,0:T(8,128)(2,1)S(1)} %prep.2.refs_0_, bf16[128,64,128]{2,1,0:T(8,128)(2,1)} %copy-done, bf16[128,64,128]{2,1,0:T(8,128)(2,1)} %copy-done.14, bf16[256,128]{1,0:T(8,128)(2,1)S(1)} %pad_maximum_fusion.refs_3_), custom_call_target="tpu_custom_call" | custom-call | flops 1073741824 | bytes 8388608 | tf_op jit(solution)/shard_map/cross/pallas_call | solution.py:85
  258.9 19.3 %reduce-scatter.15.cloned.1.call-done = bf16[32,64,128]{2,1,0:T(8,128)(2,1)} async-done(((bf16[128,64,128]{2,1,0:T(8,128)(2,1)}), bf16[32,64,128]{2,1,0:T(8,128)(2,1)}) %reduce-scatter.15.cloned.1.call-update) | async-done | bytes 524304 | tf_op jit(solution)/shard_map/reduce_scatter | solution.py:134
  278.2 45.0 %reduce-scatter.17.cloned.1.call-done = bf16[32,64,128]{2,1,0:T(8,128)(2,1)} async-done(((bf16[128,64,128]{2,1,0:T(8,128)(2,1)}), bf16[32,64,128]{2,1,0:T(8,128)(2,1)}) %reduce-scatter.17.cloned.1.call-update) | async-done | bytes 524304 | tf_op jit(solution)/shard_map/reduce_scatter | solution.py:134
  323.2 4.4 %maximum_convert_fusion = f32[3,32,128,128]{3,2,1,0:T(8,128)} fusion(bf16[1,32,64,128]{3,2,1,0:T(8,128)(2,1)} %bitcast.11, bf16[1,32,64,128]{3,2,1,0:T(8,128)(2,1)} %bitcast.10, bf16[1,32,64,128]{3,2,1,0:T(8,128)(2,1)} %bitcast.9, bf16[1,32,64,128]{3,2,1,0:T(8,128)(2,1)} %bitcast.8, bf16[1,32,64,128]{3,2,1,0:T(8,128)(2,1)} %bitcast.7, ...), kind=kLoop, calls=%fused_computation | loop fusion | flops 18874368 | bytes 9437184 | tf_op jit(solution)/shard_map/stack | solution.py:136
  (50 shorter events, 19.8 us)
Async XLA Ops:
  6.5 252.3 %reduce-scatter.7.cloned.1.call-start = ((), (), s32[]{:S(2)}) async-start(), calls=%async_computation.6 | async-start | bytes 2621440 | tf_op jit(solution)/shard_map/reduce_scatter | solution.py:134
  6.5 2.2 copy-start.1
  9.4 6.5 %copy-start.10 = (s32[128]{0:T(128)S(1)}, s32[128]{0:T(128)}, u32[]{:S(2)}) copy-start(s32[128]{0:T(128)} %live_ref.3) | copy-start | bytes 1540
  12.4 27.0 %collective-permute-start = (bf16[128,64,128]{2,1,0:T(8,128)(2,1)S(1)}, bf16[128,64,128]{2,1,0:T(8,128)(2,1)}, u32[]{:S(2)}, u32[]{:S(2)}) collective-permute-start(bf16[128,64,128]{2,1,0:T(8,128)(2,1)S(1)} %prep.2.refs_0_), channel_id=1, source_target_pairs={{0,28},{4,0},{8,4},{12,8},{16,12},{20,16},{24,20},{28,24},{1,29},{... | collective-permute-start | bytes 6291464 | tf_op jit(solution)/shard_map/ppermute | solution.py:110
  15.9 2.2 copy-start.2
  51.0 1.3 copy-start.3
  52.4 206.5 %reduce-scatter.9.cloned.1.call-start = ((), (), s32[]{:S(2)}) async-start(), calls=%async_computation.7 | async-start | bytes 2621440 | tf_op jit(solution)/shard_map/reduce_scatter | solution.py:134
  52.4 26.8 %collective-permute-start.1 = (bf16[128,64,128]{2,1,0:T(8,128)(2,1)}, bf16[128,64,128]{2,1,0:T(8,128)(2,1)S(1)}, u32[]{:S(2)}, u32[]{:S(2)}) collective-permute-start(bf16[128,64,128]{2,1,0:T(8,128)(2,1)} %copy-done), channel_id=1, source_target_pairs={{0,28},{4,0},{8,4},{12,8},{16,12},{20,16},{24,20},{28,24},{1,29},{... | collective-permute-start | bytes 6291464 | tf_op jit(solution)/shard_map/ppermute | solution.py:110
  79.3 1.4 copy-start.13
  93.6 165.3 %reduce-scatter.11.cloned.1.call-start = ((), (), s32[]{:S(2)}) async-start(), calls=%async_computation.8 | async-start | bytes 2621440 | tf_op jit(solution)/shard_map/reduce_scatter | solution.py:134
  93.7 26.8 %collective-permute-start.2 = (bf16[128,64,128]{2,1,0:T(8,128)(2,1)}, bf16[128,64,128]{2,1,0:T(8,128)(2,1)S(1)}, u32[]{:S(2)}, u32[]{:S(2)}) collective-permute-start(bf16[128,64,128]{2,1,0:T(8,128)(2,1)} %collective-permute-done.refs_2_), channel_id=1, source_target_pairs={{0,28},{4,0},{8,4},{12,8},{16,12},{20,16},{24,20},{28,24},{1,29},{... | collective-permute-start | bytes 6291464 | tf_op jit(solution)/shard_map/ppermute | solution.py:110
  120.4 1.4 copy-start.12
  133.4 1.3 copy-start.5
  134.8 124.1 %reduce-scatter.13.cloned.1.call-start = ((), (), s32[]{:S(2)}) async-start(), calls=%async_computation.9 | async-start | bytes 2621440 | tf_op jit(solution)/shard_map/reduce_scatter | solution.py:134
  134.8 27.0 %collective-permute-start.3 = (bf16[128,64,128]{2,1,0:T(8,128)(2,1)}, bf16[128,64,128]{2,1,0:T(8,128)(2,1)S(1)}, u32[]{:S(2)}, u32[]{:S(2)}) collective-permute-start(bf16[128,64,128]{2,1,0:T(8,128)(2,1)} %copy-done.13), channel_id=1, source_target_pairs={{0,28},{4,0},{8,4},{12,8},{16,12},{20,16},{24,20},{28,24},{1,29},{... | collective-permute-start | bytes 6291464 | tf_op jit(solution)/shard_map/ppermute | solution.py:110
  161.9 1.4 copy-start.11
  174.9 1.4 copy-start.6
  176.3 102.0 %reduce-scatter.15.cloned.1.call-start = ((), (), s32[]{:S(2)}) async-start(), calls=%async_computation.10 | async-start | bytes 2621440 | tf_op jit(solution)/shard_map/reduce_scatter | solution.py:134
  176.3 26.7 %collective-permute-start.4 = (bf16[128,64,128]{2,1,0:T(8,128)(2,1)}, bf16[128,64,128]{2,1,0:T(8,128)(2,1)S(1)}, u32[]{:S(2)}, u32[]{:S(2)}) collective-permute-start(bf16[128,64,128]{2,1,0:T(8,128)(2,1)} %copy-done.12), channel_id=1, source_target_pairs={{0,28},{4,0},{8,4},{12,8},{16,12},{20,16},{24,20},{28,24},{1,29},{... | collective-permute-start | bytes 6291464 | tf_op jit(solution)/shard_map/ppermute | solution.py:110
  203.0 1.4 copy-start.15
  216.0 1.4 copy-start.7
  217.4 105.8 %reduce-scatter.17.cloned.1.call-start = ((), (), s32[]{:S(2)}) async-start(), calls=%async_computation.11 | async-start | bytes 2621440 | tf_op jit(solution)/shard_map/reduce_scatter | solution.py:134
  217.5 27.0 %collective-permute-start.5 = (bf16[128,64,128]{2,1,0:T(8,128)(2,1)}, bf16[128,64,128]{2,1,0:T(8,128)(2,1)S(1)}, u32[]{:S(2)}, u32[]{:S(2)}) collective-permute-start(bf16[128,64,128]{2,1,0:T(8,128)(2,1)} %copy-done.11), channel_id=1, source_target_pairs={{0,28},{4,0},{8,4},{12,8},{16,12},{20,16},{24,20},{28,24},{1,29},{... | collective-permute-start | bytes 6291464 | tf_op jit(solution)/shard_map/ppermute | solution.py:110
  244.5 1.4 copy-start.14
  (4 other events, 4.6 us)
Sparse Core Ops, SparseCore 0:
  52.5 45.3 reduce-scatter.6
  100.2 42.8 reduce-scatter.8
  145.4 42.8 reduce-scatter.10
  190.4 42.8 reduce-scatter.12
  235.4 42.8 reduce-scatter.14
  280.4 42.8 reduce-scatter.16
